TPU v7x, 256 devices: a whole 4x4x8 slice. The times are simulated.
256 devices in a mesh: atom: 32 (over z, x_hi, core), kvec: 8 (over x_lo, y).
Axes of the slice: x: 4 (x_hi: 2, x_lo: 2; x = x_hi * 2 + x_lo), y: 4, z: 8, core: 2. Of those that a mesh axis runs over, the one named last changes fastest.
Arguments:
- scaled_coordinate_array: float32 [3, 524288], P(None, 'atom'), may hold values from 0 to 1
- particle_charge_list: float32 [524288], P('atom'), may hold values from -4 to 4
- reciprocal_triples: int32 [3, 4096], P(None, 'kvec'), may hold values from -128 to 128, as said below
Outputs:
- forces: float32 [3, 524288], P(None, 'atom')
- potential: float32 [524288], P('atom')
- energy: float32 [], replicated
Inputs may be any that keep to these rules, and one draw needn't show every extreme that they name: `reciprocal_triples`: every k-vector has a component of magnitude 64 or more.
All inputs are finite; a program needn't handle non-finite values.
Results may differ from a plain program's by a relative error of at most 0.0003.
Values sent between devices are 32-bit elements; how exact they have to be, the bound alone decides.
No kernel may reach another device: no remote copies, remote signals or barrier semaphores. Data moves between devices by JAX's collectives and lax.ppermute only.
A program may use at most 192 MiB of HBM per device.

v0:
```python
import math

import jax
import jax.numpy as jnp
from jax import lax
from jax.sharding import PartitionSpec as P


def sent_to_all(shard, axis):
    copies = jnp.broadcast_to(shard, (lax.axis_size(axis), *shard.shape))
    return lax.all_to_all(copies, axis, split_axis=0, concat_axis=0, tiled=True)


def over_copies(shard, axis):
    return sent_to_all(shard, axis).sum(axis=0)


def together(arrays, axis):
    vector, at, finished = (jnp.concatenate([a.reshape(-1) for a in arrays]), 0, [])
    total = over_copies(vector, axis)
    for a in arrays:
        finished.append(total[at : at + a.size].reshape(a.shape))
        at += a.size
    return tuple(finished)


def mode_energy_terms(reciprocal_triples):
    reciprocal_direction_table = 2.0 * math.pi * reciprocal_triples.astype(jnp.float32)
    reciprocal_norm_squared = jnp.sum(
        reciprocal_direction_table * reciprocal_direction_table, axis=0
    )
    gaussian_screening_weight = (
        4.0 * math.pi * jnp.exp(-reciprocal_norm_squared / 1600000.0) / reciprocal_norm_squared
    )
    return (reciprocal_direction_table, gaussian_screening_weight)


def phase_angle(packed, reciprocal_direction_table):
    angle = packed[0][:, None] * reciprocal_direction_table[0][None, :]
    angle = angle + packed[1][:, None] * reciprocal_direction_table[1][None, :]
    return angle + packed[2][:, None] * reciprocal_direction_table[2][None, :]


def on_device(scaled_coordinate_array, particle_charge_list, reciprocal_triples):
    reciprocal_direction_table, gaussian_screening_weight = mode_energy_terms(reciprocal_triples)
    local_atoms = scaled_coordinate_array.shape[1]
    natoms = local_atoms * lax.axis_size("atom")
    width_kvec = reciprocal_direction_table.shape[1]
    packed = jnp.concatenate([scaled_coordinate_array, particle_charge_list[None, :]], axis=0)
    tile_rows = 4096
    tile_blocks = packed.reshape(4, local_atoms // tile_rows, tile_rows).transpose(1, 0, 2)

    def make_tiles(portion):
        angle = phase_angle(portion, reciprocal_direction_table)
        return (jnp.cos(angle), jnp.sin(angle))

    cos_tile, sin_tile = lax.map(make_tiles, tile_blocks)
    cos_tile = cos_tile.reshape(local_atoms, width_kvec)
    sin_tile = sin_tile.reshape(local_atoms, width_kvec)
    largest_wave_index = lax.Precision.HIGHEST
    share_cos = jnp.dot(
        particle_charge_list,
        cos_tile,
        precision=largest_wave_index,
        preferred_element_type=jnp.float32,
    )
    share_sin = jnp.dot(
        particle_charge_list,
        sin_tile,
        precision=largest_wave_index,
        preferred_element_type=jnp.float32,
    )
    cosine_values, sine = together((share_cos, share_sin), "atom")
    partial_energy = (
        50.0
        / natoms
        * jnp.sum(gaussian_screening_weight * (cosine_values * cosine_values + sine * sine))
    )
    weighted_cos = gaussian_screening_weight * cosine_values
    weighted_sin = gaussian_screening_weight * sine
    cos_table = jnp.stack(
        [
            -weighted_sin * reciprocal_direction_table[0],
            -weighted_sin * reciprocal_direction_table[1],
            -weighted_sin * reciprocal_direction_table[2],
            weighted_cos,
        ],
        axis=1,
    )
    sine_lookup = jnp.stack(
        [
            weighted_cos * reciprocal_direction_table[0],
            weighted_cos * reciprocal_direction_table[1],
            weighted_cos * reciprocal_direction_table[2],
            weighted_sin,
        ],
        axis=1,
    )
    terms = jnp.dot(
        cos_tile, cos_table, precision=largest_wave_index, preferred_element_type=jnp.float32
    ) + jnp.dot(
        sin_tile, sine_lookup, precision=largest_wave_index, preferred_element_type=jnp.float32
    )
    terms = terms.T
    summed, energy = together((terms, partial_energy), "kvec")
    scale = 1.0 / math.sqrt(natoms)
    forces = summed[:3] * particle_charge_list[None, :] * scale
    potential = summed[3] * (400.0 * scale)
    return (forces, potential, energy)


def solution(mesh):
    return jax.shard_map(
        on_device,
        mesh=mesh,
        in_specs=(P(None, "atom"), P("atom"), P(None, "kvec")),
        out_specs=(P(None, "atom"), P("atom"), P()),
        check_vma=False,
    )
```

profile of v0, /device:TPU:2, one launch (start us, length us, event | category | flops | bytes accessed | tf_op | source)
XLA Modules:
  0.0 302.1 jit_solution(13352843346911081840)
XLA Ops:
  0.6 0.7 multiply_reduce_fusion
  1.4 1.1 maximum_bitcast_fusion
  2.5 135.3 %while.12 = (s32[]{:T(128)}, f32[4,4096,512]{2,1,0:T(8,128)}, f32[4,4096,512]{2,1,0:T(8,128)}, f32[4,4,4096]{2,1,0:T(4,128)S(1)}, f32[3,512]{1,0:T(4,128)S(1)}, /*index=5*/s32[]{:T(128)}, s32[]{:T(128)}, s32[]{}, s32[]{}) while((s32[]{:T(128)}, f32[4,4096,512]{2,1,0:T(8,128)}, f32[4,4096,512]{2,1,0:T(8,128)}, f32[4,4,4096]{2,1,0:T(4,128)S(1)}, ...), condition=%wide.region_2.3_spmd, body=%wide.region_1.2_spmd.sunk | while | flops 10485764 | bytes 16943744 | solution.py:57
  2.5 0.1 constant_dynamic-slice_fusion.4
  2.6 33.8 %sine_dynamic-update-slice_fusion.2 = (f32[4,4096,512]{2,1,0:T(8,128)}, f32[4,4096,512]{2,1,0:T(8,128)}) fusion(f32[4,4096,512]{2,1,0:T(8,128)} %get-tuple-element.125, s32[]{:T(128)} %get-tuple-element.123, f32[512]{0:T(512)S(1)} %bitcast.63, f32[4096]{0:T(1024)S(1)} %bitcast.56, f32[512]{0:T(512)S(1)} %bitcast.64, f32[4096]{0:T(1024)S(1)} %bitcast.55, ...), kind=kLoop, calls=%fused_computation.clone.1 | loop fusion | flops 10485760 | bytes 16833024 | tf_op jit(solution)/shard_map/while/body/jit(dynamic_update_index_in_dim)/dynamic_update_slice | solution.py:57
  36.4 33.7 %sine_dynamic-update-slice_fusion.2 = (f32[4,4096,512]{2,1,0:T(8,128)}, f32[4,4096,512]{2,1,0:T(8,128)}) fusion(f32[4,4096,512]{2,1,0:T(8,128)} %get-tuple-element.125, s32[]{:T(128)} %get-tuple-element.123, f32[512]{0:T(512)S(1)} %bitcast.63, f32[4096]{0:T(1024)S(1)} %bitcast.56, f32[512]{0:T(512)S(1)} %bitcast.64, f32[4096]{0:T(1024)S(1)} %bitcast.55, ...), kind=kLoop, calls=%fused_computation.clone.1 | loop fusion | flops 10485760 | bytes 16833024 | tf_op jit(solution)/shard_map/while/body/jit(dynamic_update_index_in_dim)/dynamic_update_slice | solution.py:57
  70.2 33.8 %sine_dynamic-update-slice_fusion.2 = (f32[4,4096,512]{2,1,0:T(8,128)}, f32[4,4096,512]{2,1,0:T(8,128)}) fusion(f32[4,4096,512]{2,1,0:T(8,128)} %get-tuple-element.125, s32[]{:T(128)} %get-tuple-element.123, f32[512]{0:T(512)S(1)} %bitcast.63, f32[4096]{0:T(1024)S(1)} %bitcast.56, f32[512]{0:T(512)S(1)} %bitcast.64, f32[4096]{0:T(1024)S(1)} %bitcast.55, ...), kind=kLoop, calls=%fused_computation.clone.1 | loop fusion | flops 10485760 | bytes 16833024 | tf_op jit(solution)/shard_map/while/body/jit(dynamic_update_index_in_dim)/dynamic_update_slice | solution.py:57
  104.1 33.8 %sine_dynamic-update-slice_fusion.2 = (f32[4,4096,512]{2,1,0:T(8,128)}, f32[4,4096,512]{2,1,0:T(8,128)}) fusion(f32[4,4096,512]{2,1,0:T(8,128)} %get-tuple-element.125, s32[]{:T(128)} %get-tuple-element.123, f32[512]{0:T(512)S(1)} %bitcast.63, f32[4096]{0:T(1024)S(1)} %bitcast.56, f32[512]{0:T(512)S(1)} %bitcast.64, f32[4096]{0:T(1024)S(1)} %bitcast.55, ...), kind=kLoop, calls=%fused_computation.clone.1 | loop fusion | flops 10485760 | bytes 16833024 | tf_op jit(solution)/shard_map/while/body/jit(dynamic_update_index_in_dim)/dynamic_update_slice | solution.py:57
  137.8 21.2 %fusion.22 = f32[1,512]{1,0:T(1,128)S(1)} fusion(f32[16384,512]{1,0:T(8,128)} %bitcast.50, f32[16384,1]{0,1:T(1,128)S(1)} %bitcast.58), kind=kOutput, calls=%fused_computation.43 | convolution fusion | flops 100663296 | bytes 33622016 | tf_op jit(solution)/shard_map/dot_general | solution.py:61
  159.1 21.2 %fusion.23 = f32[1,512]{1,0:T(1,128)S(1)} fusion(f32[16384,512]{1,0:T(8,128)} %bitcast.52, f32[16384,1]{0,1:T(1,128)S(1)} %bitcast.59), kind=kOutput, calls=%fused_computation.44 | convolution fusion | flops 100663296 | bytes 33622016 | tf_op jit(solution)/shard_map/dot_general | solution.py:67
  180.3 0.7 broadcast_in_dim.11
  181.0 10.6 %all-to-all-start = ((f32[32,1,1024]{2,1,0:T(1,128)}), f32[32,1,1024]{2,1,0:T(1,128)S(1)}, u32[]{:S(2)}, u32[]{:S(2)}) async-start(f32[32,1,1024]{2,1,0:T(1,128)} %broadcast_in_dim.11), calls=%async_computation | async-start | bytes 262144 | tf_op jit(solution)/shard_map/all_to_all | solution.py:11
  191.7 10.7 %all-to-all-done = f32[32,1,1024]{2,1,0:T(1,128)S(1)} async-done(((f32[32,1,1024]{2,1,0:T(1,128)}), f32[32,1,1024]{2,1,0:T(1,128)S(1)}, u32[]{:S(2)}, u32[]{:S(2)}) %all-to-all-start) | async-done | bytes 131104 | tf_op jit(solution)/shard_map/all_to_all | solution.py:11
  202.3 0.1 reduce_sum.37
  202.4 0.6 negate_multiply_fusion.2
  203.0 30.7 %fusion.1 = f32[4,16384]{1,0:T(4,128)S(1)} fusion(f32[16384,512]{1,0:T(8,128)} %bitcast.51, f32[512,1]{0,1:T(1,128)S(1)} %bitcast.66, f32[512,1]{0,1:T(1,128)S(1)} %bitcast.74, f32[512,1]{0,1:T(1,128)S(1)} %bitcast.73, f32[512,1]{0,1:T(1,128)S(1)} %bitcast.68), kind=kOutput, calls=%fused_computation.12 | convolution fusion | flops 402659328 | bytes 33824768 | tf_op jit(solution)/shard_map/dot_general | solution.py:99
  233.8 30.9 %fusion = f32[1,128,4,128]{3,2,1,0:T(4,128)S(1)} fusion(f32[4,16384]{1,0:T(4,128)S(1)} %fusion.1, f32[16384,512]{1,0:T(8,128)} %bitcast.53, f32[512,1]{0,1:T(1,128)S(1)} %bitcast.65, f32[512,1]{0,1:T(1,128)S(1)} %bitcast.72, f32[512,1]{0,1:T(1,128)S(1)} %bitcast.71, f32[512,1]{0,1:T(1,128)S(1)} %bitcast.67), kind=kOutput, calls=%fused_computation.7 | convolution fusion | flops 402724864 | bytes 34086912 | tf_op jit(solution)/shard_map/dot_general | solution.py:101
  265.4 1.1 broadcast_in_dim.12
  266.5 32.0 %all_to_all.12 = f32[8,1,65537]{2,1,0:T(1,128)S(1)} all-to-all(f32[8,1,65537]{2,1,0:T(1,128)S(1)} %broadcast_in_dim.12), channel_id=1, replica_groups=mesh['atom'=32,'kvec'=8] {'kvec'}, dimensions={0} | all-to-all | bytes 4194368 | tf_op jit(solution)/shard_map/all_to_all | solution.py:11
  298.5 1.5 reduce_sum.39
  300.0 0.6 slice_multiply_fusion
  300.7 0.5 slice.71
  301.2 0.1 slice.63
  301.3 0.8 multiply_multiply_fusion
  (17 shorter events, 0.2 us)
Async XLA Ops:
  2.5 135.3 %copy-start = (f32[16384]{0:T(1024)S(1)}, f32[16384]{0:T(1024)}, u32[]{:S(2)}) copy-start(f32[16384]{0:T(1024)} %param.6) | copy-start | bytes 196612
  181.0 21.3 %all-to-all-start = ((f32[32,1,1024]{2,1,0:T(1,128)}), f32[32,1,1024]{2,1,0:T(1,128)S(1)}, u32[]{:S(2)}, u32[]{:S(2)}) async-start(f32[32,1,1024]{2,1,0:T(1,128)} %broadcast_in_dim.11), calls=%async_computation | async-start | bytes 262144 | tf_op jit(solution)/shard_map/all_to_all | solution.py:11
where the time goes:
time: 303 us; the launch traced here: 302 us
  other arithmetic  141 us (47%)
  matrix products  104 us (34%)
  blocking collectives  32 us (11%)
  waiting for transfers between devices  10.7 us (4%)
  starting transfers between devices  10.6 us (3%)
    dynamic_update_slice x4, other arithmetic, on_device(): cos_tile, sin_tile = lax.map(make_tiles, tile_blocks)  135 us
    all_to_all x1, blocking collectives, sent_to_all(): return lax.all_to_all(copies, axis, split_axis=0, concat_axis=0, tiled=True)  32 us
    dot_general x1, matrix products, on_device(): jnp.dot(sin_tile, sine_lookup, precision=largest_wave_index, preferred_el...  30.9 us
    dot_general x1, matrix products, on_device(): jnp.dot(cos_tile, cos_table, precision=largest_wave_index, preferred_elem...  30.7 us
    dot_general x1, matrix products, on_device(): jnp.dot(particle_charge_list, cos_tile, precision=largest_wave_index, pre...  21.2 us
    dot_general x1, matrix products, on_device(): jnp.dot(particle_charge_list, sin_tile, precision=largest_wave_index, pre...  21.2 us
    all_to_all x1, waiting for transfers between devices, sent_to_all(): return lax.all_to_all(copies, axis, split_axis=0, concat_axis=0, tiled=True)  10.7 us
    all_to_all x1, starting transfers between devices, sent_to_all(): return lax.all_to_all(copies, axis, split_axis=0, concat_axis=0, tiled=True)  10.6 us
  transfers between devices with their start and end apart: 1, of which 1 were waited for; matrix products, arithmetic and copies ran while one was open for 0% of the time, Pallas kernels for 0%

commit v1 on v0

v1 whole, which is shorter than its diff:
```python
import math

import jax
import jax.numpy as jnp
from jax import lax
from jax.experimental import pallas as pl
from jax.experimental.pallas import tpu as pltpu
from jax.sharding import PartitionSpec as P

TOP = 128
BLOCK = 2048
ROWS = BLOCK // 128
CHUNK = 128
MIB = 1 << 20


def phases_kernel(idx_ref, xyz_ref, q_ref, e_ref, s_ref, xc, xs, yc, ys, zc, zs, acc):
    b = pl.program_id(0)
    kc = pl.program_id(1)

    @pl.when((b == 0) & (kc == 0))
    def _():
        def clear(i, carry):
            acc[i] = jnp.zeros((8, 128), jnp.float32)
            return carry

        lax.fori_loop(0, acc.shape[0], clear, 0, unroll=8)

    @pl.when(kc == 0)
    def _():
        base = []
        for d in range(3):
            x = xyz_ref[d]
            angle = (2.0 * math.pi) * (x - jnp.round(x))
            base.append((jnp.cos(angle), jnp.sin(angle)))

        def put(h, state):
            (c0, s0), (c1, s1), (c2, s2) = state
            xc[h] = c0
            xs[h] = s0
            yc[h] = c1
            ys[TOP + h] = s1
            ys[TOP - h] = -s1
            zc[h] = c2
            zs[TOP + h] = s2
            zs[TOP - h] = -s2

        def step(h, state):
            put(h, state)
            return tuple(
                (c * bc - s * bs, c * bs + s * bc) for (c, s), (bc, bs) in zip(state, base)
            )

        one = jnp.ones((ROWS, 128), jnp.float32)
        zero = jnp.zeros((ROWS, 128), jnp.float32)
        put(0, ((one, zero),) * 3)
        lax.fori_loop(1, TOP + 1, step, tuple(base), unroll=4)

    q = q_ref[...]

    def mode(i, carry):
        k = kc * CHUNK + i
        h = idx_ref[0, k]
        cx, sx = xc[h], xs[h]
        cy, sy = yc[idx_ref[1, k]], ys[idx_ref[2, k]]
        cz, sz = zc[idx_ref[3, k]], zs[idx_ref[4, k]]
        cp = cx * cy - sx * sy
        sp = cx * sy + sx * cy
        c = cp * cz - sp * sz
        s = cp * sz + sp * cz
        e_ref[0, i, 0] = c
        e_ref[0, i, 1] = s
        qc = q * c
        qs = q * s
        acc[2 * k] += qc[:8] + qc[8:]
        acc[2 * k + 1] += qs[:8] + qs[8:]
        return carry

    lax.fori_loop(0, CHUNK, mode, 0, unroll=4)

    @pl.when((b == pl.num_programs(0) - 1) & (kc == pl.num_programs(1) - 1))
    def _():
        n = acc.shape[0]
        rows = acc[:, 0, :]
        for r in range(1, 8):
            rows = rows + acc[:, r, :]
        ones = jnp.ones((8, 128), jnp.float32)
        s_ref[...] = lax.dot_general(
            ones,
            rows,
            (((1,), (1,)), ((), ())),
            precision=lax.Precision.HIGHEST,
            preferred_element_type=jnp.float32,
        )


def response_kernel(w_ref, e_ref, o_ref):
    kc = pl.program_id(1)

    @pl.when(kc == 0)
    def _():
        o_ref[0, : 4 * ROWS] = jnp.zeros((4 * ROWS, 128), jnp.float32)
        o_ref[0, 4 * ROWS :] = jnp.full((8, 128), w_ref[5, 0], jnp.float32)

    def mode(i, carry):
        f0, f1, f2, p = carry
        k = kc * CHUNK + i
        wr, wi = w_ref[0, k], w_ref[1, k]
        c = e_ref[0, i, 0]
        s = e_ref[0, i, 1]
        p = p + (wr * c + wi * s)
        g = wr * s - wi * c
        return (f0 + w_ref[2, k] * g, f1 + w_ref[3, k] * g, f2 + w_ref[4, k] * g, p)

    start = tuple(o_ref[0, ROWS * c : ROWS * (c + 1)] for c in range(4))
    done = lax.fori_loop(0, CHUNK, mode, start, unroll=4)
    for c in range(4):
        o_ref[0, ROWS * c : ROWS * (c + 1)] = done[c]


def on_device(scaled_coordinate_array, particle_charge_list, reciprocal_triples):
    local_atoms = scaled_coordinate_array.shape[1]
    modes = reciprocal_triples.shape[1]
    n_atom = lax.axis_size("atom")
    n_kvec = lax.axis_size("kvec")
    natoms = local_atoms * n_atom
    blocks = local_atoms // BLOCK
    chunks = modes // CHUNK

    triples = reciprocal_triples * jnp.where(reciprocal_triples[0:1] < 0, -1, 1)
    table = 2.0 * math.pi * triples.astype(jnp.float32)
    norm = jnp.sum(table * table, axis=0)
    damping = 4.0 * math.pi * jnp.exp(-norm / 1600000.0) / norm
    idx = jnp.stack(
        [
            triples[0],
            jnp.abs(triples[1]),
            triples[1] + TOP,
            jnp.abs(triples[2]),
            triples[2] + TOP,
        ]
    )
    xyz = scaled_coordinate_array.reshape(3, local_atoms // 128, 128)
    q = particle_charge_list.reshape(local_atoms // 128, 128)

    e, s = pl.pallas_call(
        phases_kernel,
        grid=(blocks, chunks),
        in_specs=[
            pl.BlockSpec(memory_space=pltpu.SMEM),
            pl.BlockSpec((3, ROWS, 128), lambda b, c: (0, b, 0)),
            pl.BlockSpec((ROWS, 128), lambda b, c: (b, 0)),
        ],
        out_specs=[
            pl.BlockSpec((1, CHUNK, 2, ROWS, 128), lambda b, c: (b, c, 0, 0, 0)),
            pl.BlockSpec((8, 2 * modes), lambda b, c: (0, 0)),
        ],
        out_shape=[
            jax.ShapeDtypeStruct((blocks, modes, 2, ROWS, 128), jnp.float32),
            jax.ShapeDtypeStruct((8, 2 * modes), jnp.float32),
        ],
        scratch_shapes=[
            pltpu.VMEM((TOP + 1, ROWS, 128), jnp.float32),
            pltpu.VMEM((TOP + 1, ROWS, 128), jnp.float32),
            pltpu.VMEM((TOP + 1, ROWS, 128), jnp.float32),
            pltpu.VMEM((2 * TOP + 1, ROWS, 128), jnp.float32),
            pltpu.VMEM((TOP + 1, ROWS, 128), jnp.float32),
            pltpu.VMEM((2 * TOP + 1, ROWS, 128), jnp.float32),
            pltpu.VMEM((2 * modes, 8, 128), jnp.float32),
        ],
        compiler_params=pltpu.CompilerParams(
            dimension_semantics=("arbitrary", "arbitrary"), vmem_limit_bytes=40 * MIB
        ),
    )(idx, xyz, q)

    share = jnp.broadcast_to(s[0:1], (n_atom, 2 * modes))
    total = lax.all_to_all(share, "atom", 0, 0, tiled=True).sum(axis=0)
    total = total.reshape(modes, 2)
    cosine, sine = total[:, 0], total[:, 1]
    partial_energy = 50.0 / natoms * jnp.sum(damping * (cosine * cosine + sine * sine))
    w = jnp.concatenate(
        [
            (damping * cosine)[None],
            (damping * sine)[None],
            table,
            jnp.broadcast_to(partial_energy, (1, modes)),
        ]
    )

    terms = pl.pallas_call(
        response_kernel,
        grid=(blocks, chunks),
        in_specs=[
            pl.BlockSpec(memory_space=pltpu.SMEM),
            pl.BlockSpec((1, CHUNK, 2, ROWS, 128), lambda b, c: (b, c, 0, 0, 0)),
        ],
        out_specs=pl.BlockSpec((1, 4 * ROWS + 8, 128), lambda b, c: (b, 0, 0)),
        out_shape=jax.ShapeDtypeStruct((blocks, 4 * ROWS + 8, 128), jnp.float32),
        compiler_params=pltpu.CompilerParams(
            dimension_semantics=("arbitrary", "arbitrary"), vmem_limit_bytes=40 * MIB
        ),
    )(w, e)

    mine = lax.all_to_all(terms, "kvec", 0, 0, tiled=True).sum(axis=0)
    energy = mine[4 * ROWS, 0]
    copies = jnp.broadcast_to(mine[None, : 4 * ROWS], (n_kvec, 4 * ROWS, 128))
    summed = lax.all_to_all(copies, "kvec", 0, 0, tiled=True)
    summed = summed.reshape(n_kvec, 4, BLOCK).transpose(1, 0, 2).reshape(4, local_atoms)
    scale = 1.0 / math.sqrt(natoms)
    forces = summed[:3] * particle_charge_list[None, :] * scale
    potential = summed[3] * (400.0 * scale)
    return (forces, potential, energy)


def solution(mesh):
    return jax.shard_map(
        on_device,
        mesh=mesh,
        in_specs=(P(None, "atom"), P("atom"), P(None, "kvec")),
        out_specs=(P(None, "atom"), P("atom"), P()),
        check_vma=False,
    )
```

time: 303 us -> 153 us (0.50)
  other arithmetic: 141 us -> 4.18 us
  matrix products: 104 us -> 0 us
  Pallas kernels: 0 us -> 98.7 us
  blocking collectives: 32 us -> 12.6 us
  waiting for transfers between devices: 10.7 us -> 16 us
  starting transfers between devices: 10.6 us -> 15.2 us
    dynamic_update_slice x4 -> x0, other arithmetic: 135 us -> none  [on_device(): cos_tile, sin_tile = lax.map(make_tiles, tile_blocks)]
    dot_general x4 -> x0, matrix products: 104 us -> none  [the longest x1 30.9 us: on_device(): jnp.dot(sin_tile, sine_lookup, precision=largest_wave_index, preferred_el...]
    pallas_call x0 -> x2, Pallas kernels: none -> 98.7 us  [the longest x1 56.2 us: on_device(): pl.pallas_call(phases_kernel, grid=(blocks, chunks), in_specs=[pl.BlockSp...]
    all_to_all x1, blocking collectives: 32 us -> 12.6 us  [on_device(): mine = lax.all_to_all(terms, 'kvec', 0, 0, tiled=True).sum(axis=0)]
    all_to_all x1 -> x2, waiting for transfers between devices: 10.7 us -> 16 us  [the longest x1 10.7 us: on_device(): total = lax.all_to_all(share, 'atom', 0, 0, tiled=True).sum(axis=0)]
    all_to_all x1 -> x2, starting transfers between devices: 10.6 us -> 15.2 us  [the longest x1 10.4 us: on_device(): total = lax.all_to_all(share, 'atom', 0, 0, tiled=True).sum(axis=0)]
  transfers between devices with their start and end apart: 1 -> 2, of which waited for: 1 -> 2; matrix products, arithmetic and copies ran while one was open for 0% -> 0% of each run, Pallas kernels for 0% -> 0%
where the time goes in v1:
time: 153 us; the launch traced here: 152 us
  Pallas kernels  98.7 us (65%)
  waiting for transfers between devices  16 us (10%)
  starting transfers between devices  15.2 us (10%)
  blocking collectives  12.6 us (8%)
  other arithmetic  4.18 us (3%)
  local copies, waits for them, and re-layouts  4.17 us (3%)
    pallas_call x1, Pallas kernels, on_device(): pl.pallas_call(phases_kernel, grid=(blocks, chunks), in_specs=[pl.BlockSp...  56.2 us
    pallas_call x1, Pallas kernels, on_device(): pl.pallas_call(response_kernel, grid=(blocks, chunks), in_specs=[pl.Block...  42.5 us
    all_to_all x1, blocking collectives, on_device(): mine = lax.all_to_all(terms, 'kvec', 0, 0, tiled=True).sum(axis=0)  12.6 us
    all_to_all x1, waiting for transfers between devices, on_device(): total = lax.all_to_all(share, 'atom', 0, 0, tiled=True).sum(axis=0)  10.7 us
    all_to_all x1, starting transfers between devices, on_device(): total = lax.all_to_all(share, 'atom', 0, 0, tiled=True).sum(axis=0)  10.4 us
    all_to_all x1, waiting for transfers between devices, on_device(): summed = lax.all_to_all(copies, 'kvec', 0, 0, tiled=True)  5.33 us
    all_to_all x1, starting transfers between devices, on_device(): summed = lax.all_to_all(copies, 'kvec', 0, 0, tiled=True)  4.8 us
  transfers between devices with their start and end apart: 2, of which 2 were waited for; matrix products, arithmetic and copies ran while one was open for 0% of the time, Pallas kernels for 0%

profile of v1, /device:TPU:2, one launch (start us, length us, event | category | flops | bytes accessed | tf_op | source)
XLA Modules:
  0.0 152.2 jit_solution(13159075933710780844)
XLA Ops:
  0.6 0.0 copy-start.1
  0.6 0.7 compare_select_fusion
  1.4 0.7 multiply_reduce_fusion
  2.1 1.0 copy.10
  3.1 0.8 copy-done
  4.0 56.2 %shard_map.58 = (f32[8,512,2,16,128]{4,3,2,1,0:T(8,128)}, f32[8,1024]{1,0:T(8,128)S(1)}) custom-call(s32[5,512]{1,0:T(8,128)S(1)} %stack.2.idx_ref, f32[3,128,128]{2,1,0:T(8,128)S(1)} %bitcast.16, f32[128,128]{1,0:T(8,128)S(1)} %bitcast.17), custom_call_target="tpu_custom_call" | custom-call | tf_op jit(solution)/shard_map/pallas_call | solution.py:146
  60.1 0.7 broadcast_in_dim.27
  60.9 10.4 %all-to-all-start = ((f32[32,1,1024]{2,1,0:T(1,128)}), f32[32,1,1024]{2,1,0:T(1,128)S(1)}, u32[]{:S(2)}, u32[]{:S(2)}) async-start(f32[32,1,1024]{2,1,0:T(1,128)} %broadcast_in_dim.27), calls=%async_computation | async-start | bytes 262144 | tf_op jit(solution)/shard_map/all_to_all | solution.py:177
  71.3 10.7 %all-to-all-done = f32[32,1,1024]{2,1,0:T(1,128)S(1)} async-done(((f32[32,1,1024]{2,1,0:T(1,128)}), f32[32,1,1024]{2,1,0:T(1,128)S(1)}, u32[]{:S(2)}, u32[]{:S(2)}) %all-to-all-start) | async-done | bytes 131104 | tf_op jit(solution)/shard_map/all_to_all | solution.py:177
  82.0 0.1 reduce_sum.40
  82.1 0.2 reshape.80
  82.3 0.4 add_reduce_fusion
  82.7 0.6 multiply_reduce_fusion.1
  83.9 0.1 pad.3.clone
  84.0 0.1 maximum_maximum_fusion.w_ref
  84.1 42.5 %shard_map.59 = f32[8,72,128]{2,1,0:T(8,128)S(1)} custom-call(f32[6,512]{1,0:T(8,128)S(1)} %maximum_maximum_fusion.w_ref, f32[8,512,2,16,128]{4,3,2,1,0:T(8,128)} %get-tuple-element.6.e_ref), custom_call_target="tpu_custom_call" | custom-call | tf_op jit(solution)/shard_map/pallas_call | solution.py:190
  126.6 12.6 %all_to_all.16 = f32[8,72,128]{2,1,0:T(8,128)S(1)} all-to-all(f32[8,72,128]{2,1,0:T(8,128)S(1)} %shard_map.59), channel_id=1, replica_groups=mesh['atom'=32,'kvec'=8] {'kvec'}, dimensions={0} | all-to-all | bytes 589824 | tf_op jit(solution)/shard_map/all_to_all | solution.py:204
  139.2 0.7 broadcast_in_dim.29
  140.0 4.8 %all-to-all-start.2 = ((f32[8,64,128]{2,1,0:T(8,128)}), f32[8,64,128]{2,1,0:T(8,128)S(1)}, u32[]{:S(2)}, u32[]{:S(2)}) async-start(f32[8,64,128]{2,1,0:T(8,128)} %broadcast_in_dim.29), calls=%async_computation.2 | async-start | bytes 524288 | tf_op jit(solution)/shard_map/all_to_all | solution.py:207
  144.8 0.5 slice.62
  145.3 5.3 %all-to-all-done.2 = f32[8,64,128]{2,1,0:T(8,128)S(1)} async-done(((f32[8,64,128]{2,1,0:T(8,128)}), f32[8,64,128]{2,1,0:T(8,128)S(1)}, u32[]{:S(2)}, u32[]{:S(2)}) %all-to-all-start.2) | async-done | bytes 262176 | tf_op jit(solution)/shard_map/all_to_all | solution.py:207
  150.6 0.1 reshape.81
  150.7 0.7 slice_multiply_fusion
  151.4 0.8 multiply_multiply_fusion
  (10 shorter events, 0.1 us)
Async XLA Ops:
  0.6 150.8 %copy-start.1 = (f32[16384]{0:T(1024)S(1)}, f32[16384]{0:T(1024)}, u32[]{:S(2)}) copy-start(f32[16384]{0:T(1024)} %param.4) | copy-start | bytes 196612
  3.1 0.8 copy-start
  60.9 21.1 %all-to-all-start = ((f32[32,1,1024]{2,1,0:T(1,128)}), f32[32,1,1024]{2,1,0:T(1,128)S(1)}, u32[]{:S(2)}, u32[]{:S(2)}) async-start(f32[32,1,1024]{2,1,0:T(1,128)} %broadcast_in_dim.27), calls=%async_computation | async-start | bytes 262144 | tf_op jit(solution)/shard_map/all_to_all | solution.py:177
  140.0 10.6 %all-to-all-start.2 = ((f32[8,64,128]{2,1,0:T(8,128)}), f32[8,64,128]{2,1,0:T(8,128)S(1)}, u32[]{:S(2)}, u32[]{:S(2)}) async-start(f32[8,64,128]{2,1,0:T(8,128)} %broadcast_in_dim.29), calls=%async_computation.2 | async-start | bytes 524288 | tf_op jit(solution)/shard_map/all_to_all | solution.py:207

commit v2 on v1

v2 whole, which is shorter than its diff:
```python
import math

import jax
import jax.numpy as jnp
from jax import lax
from jax.experimental import pallas as pl
from jax.experimental.pallas import tpu as pltpu
from jax.sharding import PartitionSpec as P

TOP = 128
BLOCK = 4096
ROWS = BLOCK // 128
SPLIT = 4
PART = 32
CHUNK = SPLIT * PART
HALF = ROWS // 2
MIB = 1 << 20


def rows_of(ref, start):
    return ref[pl.ds(pl.multiple_of(start, ROWS), ROWS), :]


def phases_kernel(idx_ref, xyz_ref, q_ref, *refs):
    e_refs = refs[:SPLIT]
    s_ref, xc, xs, yc, ys, zc, zs, acc = refs[SPLIT:]
    b = pl.program_id(0)
    kc = pl.program_id(1)

    @pl.when((b == 0) & (kc == 0))
    def _():
        def clear(i, carry):
            acc[i] = jnp.zeros((8, 128), jnp.float32)
            return carry

        lax.fori_loop(0, acc.shape[0], clear, 0, unroll=8)

    @pl.when(kc == 0)
    def _():
        for part in range(2):
            low = part * HALF

            def row(h):
                return pl.ds(pl.multiple_of(h * ROWS + low, 8), HALF)

            base = []
            for d in range(3):
                x = xyz_ref[d, low : low + HALF]
                angle = (2.0 * math.pi) * (x - jnp.round(x))
                base.append((jnp.cos(angle), jnp.sin(angle)))

            def put(h, state):
                (c0, s0), (c1, s1), (c2, s2) = state
                xc[row(h)] = c0
                xs[row(h)] = s0
                yc[row(h)] = c1
                ys[row(TOP + h)] = s1
                ys[row(TOP - h)] = -s1
                zc[row(h)] = c2
                zs[row(TOP + h)] = s2
                zs[row(TOP - h)] = -s2

            def step(h, state):
                put(h, state)
                return tuple(
                    (c * bc - s * bs, c * bs + s * bc) for (c, s), (bc, bs) in zip(state, base)
                )

            one = jnp.ones((HALF, 128), jnp.float32)
            zero = jnp.zeros((HALF, 128), jnp.float32)
            put(0, ((one, zero),) * 3)
            lax.fori_loop(1, TOP + 1, step, tuple(base), unroll=4)

    q = q_ref[...]

    def eighths(v):
        return (v[0:8] + v[8:16]) + (v[16:24] + v[24:32])

    for j in range(SPLIT):

        def mode(i, carry, j=j):
            k = kc * CHUNK + j * PART + i
            at = k * 5
            h = idx_ref[at]
            cx, sx = rows_of(xc, h), rows_of(xs, h)
            cy, sy = rows_of(yc, idx_ref[at + 1]), rows_of(ys, idx_ref[at + 2])
            cz, sz = rows_of(zc, idx_ref[at + 3]), rows_of(zs, idx_ref[at + 4])
            cp = cx * cy - sx * sy
            sp = cx * sy + sx * cy
            c = cp * cz - sp * sz
            s = cp * sz + sp * cz
            e_refs[j][0, i, 0] = c
            e_refs[j][0, i, 1] = s
            acc[2 * k] += eighths(q * c)
            acc[2 * k + 1] += eighths(q * s)
            return carry

        lax.fori_loop(0, PART, mode, 0, unroll=8)

    @pl.when((b == pl.num_programs(0) - 1) & (kc == pl.num_programs(1) - 1))
    def _():
        rows = acc[:, 0, :]
        for r in range(1, 8):
            rows = rows + acc[:, r, :]
        ones = jnp.ones((8, 128), jnp.float32)
        s_ref[...] = lax.dot_general(
            ones,
            rows,
            (((1,), (1,)), ((), ())),
            precision=lax.Precision.HIGHEST,
            preferred_element_type=jnp.float32,
        )


def response_kernel(w_ref, *refs):
    e_refs = refs[:SPLIT]
    o_ref = refs[SPLIT]
    kc = pl.program_id(1)
    modes = (w_ref.shape[0] - 1) // 5

    @pl.when(kc == 0)
    def _():
        for t in range(2):
            o_ref[t, : 4 * HALF] = jnp.zeros((4 * HALF, 128), jnp.float32)
            o_ref[t, 4 * HALF :] = jnp.full((8, 128), w_ref[5 * modes], jnp.float32)

    def mine(c):
        part = slice(HALF * c, HALF * (c + 1))
        return jnp.concatenate([o_ref[0, part], o_ref[1, part]], axis=0)

    state = tuple(mine(c) for c in range(4))
    for j in range(SPLIT):

        def mode(i, carry, j=j):
            f0, f1, f2, p = carry
            at = (kc * CHUNK + j * PART + i) * 5
            wr, wi = w_ref[at], w_ref[at + 1]
            c = e_refs[j][0, i, 0]
            s = e_refs[j][0, i, 1]
            p = p + (wr * c + wi * s)
            g = wr * s - wi * c
            return (f0 + w_ref[at + 2] * g, f1 + w_ref[at + 3] * g, f2 + w_ref[at + 4] * g, p)

        state = lax.fori_loop(0, PART, mode, state, unroll=8)
    for c in range(4):
        o_ref[0, HALF * c : HALF * (c + 1)] = state[c][:HALF]
        o_ref[1, HALF * c : HALF * (c + 1)] = state[c][HALF:]


def on_device(scaled_coordinate_array, particle_charge_list, reciprocal_triples):
    local_atoms = scaled_coordinate_array.shape[1]
    modes = reciprocal_triples.shape[1]
    n_atom = lax.axis_size("atom")
    n_kvec = lax.axis_size("kvec")
    natoms = local_atoms * n_atom
    blocks = local_atoms // BLOCK
    chunks = modes // CHUNK

    triples = reciprocal_triples * jnp.where(reciprocal_triples[0:1] < 0, -1, 1)
    table = 2.0 * math.pi * triples.astype(jnp.float32)
    norm = jnp.sum(table * table, axis=0)
    damping = 4.0 * math.pi * jnp.exp(-norm / 1600000.0) / norm
    idx = ROWS * jnp.stack(
        [
            triples[0],
            jnp.abs(triples[1]),
            triples[1] + TOP,
            jnp.abs(triples[2]),
            triples[2] + TOP,
        ],
        axis=1,
    ).reshape(5 * modes)
    xyz = scaled_coordinate_array.reshape(3, local_atoms // 128, 128)
    q = particle_charge_list.reshape(local_atoms // 128, 128)

    e_spec = pl.BlockSpec((1, PART, 2, ROWS, 128), lambda b, c: (b, c, 0, 0, 0))
    e_shape = jax.ShapeDtypeStruct((blocks, modes // SPLIT, 2, ROWS, 128), jnp.float32)
    *e, s = pl.pallas_call(
        phases_kernel,
        grid=(blocks, chunks),
        in_specs=[
            pl.BlockSpec(memory_space=pltpu.SMEM),
            pl.BlockSpec((3, ROWS, 128), lambda b, c: (0, b, 0)),
            pl.BlockSpec((ROWS, 128), lambda b, c: (b, 0)),
        ],
        out_specs=[e_spec] * SPLIT + [pl.BlockSpec((8, 2 * modes), lambda b, c: (0, 0))],
        out_shape=[e_shape] * SPLIT + [jax.ShapeDtypeStruct((8, 2 * modes), jnp.float32)],
        scratch_shapes=[
            pltpu.VMEM(((TOP + 1) * ROWS, 128), jnp.float32),
            pltpu.VMEM(((TOP + 1) * ROWS, 128), jnp.float32),
            pltpu.VMEM(((TOP + 1) * ROWS, 128), jnp.float32),
            pltpu.VMEM(((2 * TOP + 1) * ROWS, 128), jnp.float32),
            pltpu.VMEM(((TOP + 1) * ROWS, 128), jnp.float32),
            pltpu.VMEM(((2 * TOP + 1) * ROWS, 128), jnp.float32),
            pltpu.VMEM((2 * modes, 8, 128), jnp.float32),
        ],
        compiler_params=pltpu.CompilerParams(
            dimension_semantics=("arbitrary", "arbitrary"), vmem_limit_bytes=48 * MIB
        ),
    )(idx, xyz, q)

    share = jnp.broadcast_to(s[0:1], (n_atom, 2 * modes))
    total = lax.all_to_all(share, "atom", 0, 0, tiled=True).sum(axis=0)
    total = total.reshape(modes, 2)
    cosine, sine = total[:, 0], total[:, 1]
    partial_energy = 50.0 / natoms * jnp.sum(damping * (cosine * cosine + sine * sine))
    w = jnp.concatenate([(damping * cosine)[None], (damping * sine)[None], table])
    w = jnp.concatenate([w.T.reshape(5 * modes), partial_energy.reshape(1)])

    terms = pl.pallas_call(
        response_kernel,
        grid=(blocks, chunks),
        in_specs=[pl.BlockSpec(memory_space=pltpu.SMEM)] + [e_spec] * SPLIT,
        out_specs=pl.BlockSpec((2, 4 * HALF + 8, 128), lambda b, c: (b, 0, 0)),
        out_shape=jax.ShapeDtypeStruct((n_kvec, 4 * HALF + 8, 128), jnp.float32),
        compiler_params=pltpu.CompilerParams(
            dimension_semantics=("arbitrary", "arbitrary"), vmem_limit_bytes=48 * MIB
        ),
    )(w, *e)

    own = lax.all_to_all(terms, "kvec", 0, 0, tiled=True).sum(axis=0)
    energy = own[4 * HALF, 0]
    copies = jnp.broadcast_to(own[None, : 4 * HALF], (n_kvec, 4 * HALF, 128))
    summed = lax.all_to_all(copies, "kvec", 0, 0, tiled=True)
    summed = summed.reshape(n_kvec, 4, HALF * 128).transpose(1, 0, 2).reshape(4, local_atoms)
    scale = 1.0 / math.sqrt(natoms)
    forces = summed[:3] * particle_charge_list[None, :] * scale
    potential = summed[3] * (400.0 * scale)
    return (forces, potential, energy)


def solution(mesh):
    return jax.shard_map(
        on_device,
        mesh=mesh,
        in_specs=(P(None, "atom"), P("atom"), P(None, "kvec")),
        out_specs=(P(None, "atom"), P("atom"), P()),
        check_vma=False,
    )
```

time: 153 us -> 123 us (0.80)
  Pallas kernels: 98.7 us -> 68.6 us
    pallas_call x1, Pallas kernels: 56.2 us -> 39.9 us  [on_device(): pl.pallas_call(phases_kernel, grid=(blocks, chunks), in_specs=[pl.BlockSp...]
    pallas_call x1, Pallas kernels: 42.5 us -> 28.8 us  [on_device(): pl.pallas_call(response_kernel, grid=(blocks, chunks), in_specs=[pl.Block...]
where the time goes in v2:
time: 123 us
  Pallas kernels  68.6 us (56%)
  waiting for transfers between devices  16 us (13%)
  starting transfers between devices  15.2 us (12%)
  blocking collectives  12.6 us (10%)
  local copies, waits for them, and re-layouts  4.79 us (4%)
  other arithmetic  4.1 us (3%)
  between operations  1.41 us (1%)
    pallas_call x1, Pallas kernels, on_device(): pl.pallas_call(phases_kernel, grid=(blocks, chunks), in_specs=[pl.BlockSp...  39.9 us
    pallas_call x1, Pallas kernels, on_device(): pl.pallas_call(response_kernel, grid=(blocks, chunks), in_specs=[pl.Block...  28.8 us
    all_to_all x1, blocking collectives, on_device(): own = lax.all_to_all(terms, 'kvec', 0, 0, tiled=True).sum(axis=0)  12.6 us
    all_to_all x1, waiting for transfers between devices, on_device(): total = lax.all_to_all(share, 'atom', 0, 0, tiled=True).sum(axis=0)  10.7 us
    all_to_all x1, starting transfers between devices, on_device(): total = lax.all_to_all(share, 'atom', 0, 0, tiled=True).sum(axis=0)  10.4 us
    all_to_all x1, waiting for transfers between devices, on_device(): summed = lax.all_to_all(copies, 'kvec', 0, 0, tiled=True)  5.33 us
    all_to_all x1, starting transfers between devices, on_device(): summed = lax.all_to_all(copies, 'kvec', 0, 0, tiled=True)  4.8 us
  transfers between devices with their start and end apart: 2, of which 2 were waited for; matrix products, arithmetic and copies ran while one was open for 0% of the time, Pallas kernels for 0%

profile of v2, /device:TPU:2, one launch (start us, length us, event | category | flops | bytes accessed | tf_op | source)
XLA Modules:
  0.0 122.7 jit_solution(2008448971368108198)
XLA Ops:
  0.6 0.7 compare_select_fusion
  1.3 0.7 convert_multiply_fusion
  2.1 1.0 copy.16
  3.1 0.1 copy.10
  3.2 0.2 mul.112.idx_ref
  3.4 0.8 copy-done
  4.3 39.9 %shard_map.58 = (f32[4,128,2,32,128]{4,3,2,1,0:T(8,128)}, f32[4,128,2,32,128]{4,3,2,1,0:T(8,128)}, f32[4,128,2,32,128]{4,3,2,1,0:T(8,128)}, f32[4,128,2,32,128]{4,3,2,1,0:T(8,128)}, f32[8,1024]{1,0:T(8,128)S(1)}) custom-call(s32[2560]{0:T(1024)S(1)} %mul.112.idx_ref, f32[3,128,128]{2,1,0:T(8,128)S(1)} %bitcast.28, f32[128,128]{1,0:T(8,128)S(1)} %bitcast.29), custom_call_target="tpu_custom_call" | custom-call | tf_op jit(solution)/shard_map/pallas_call | solution.py:178
  44.1 0.7 broadcast_in_dim.24
  44.9 10.4 %all-to-all-start = ((f32[32,1,1024]{2,1,0:T(1,128)}), f32[32,1,1024]{2,1,0:T(1,128)S(1)}, u32[]{:S(2)}, u32[]{:S(2)}) async-start(f32[32,1,1024]{2,1,0:T(1,128)} %broadcast_in_dim.24), calls=%async_computation | async-start | bytes 262144 | tf_op jit(solution)/shard_map/all_to_all | solution.py:203
  55.3 10.7 %all-to-all-done = f32[32,1,1024]{2,1,0:T(1,128)S(1)} async-done(((f32[32,1,1024]{2,1,0:T(1,128)}), f32[32,1,1024]{2,1,0:T(1,128)S(1)}, u32[]{:S(2)}, u32[]{:S(2)}) %all-to-all-start) | async-done | bytes 131104 | tf_op jit(solution)/shard_map/all_to_all | solution.py:203
  66.0 0.1 reduce_sum.40
  66.1 0.2 reshape.135
  66.3 0.4 slice_reduce_fusion.1
  66.6 0.6 multiply_reduce_fusion.1
  67.3 0.1 copy.12
  67.5 0.2 reshape.136
  68.4 28.8 %shard_map.59 = f32[8,72,128]{2,1,0:T(8,128)S(1)} custom-call(f32[2561]{0:T(1024)S(1)} %pad_maximum_fusion.w_ref, f32[4,128,2,32,128]{4,3,2,1,0:T(8,128)} %get-tuple-element.9.refs_0_, f32[4,128,2,32,128]{4,3,2,1,0:T(8,128)} %get-tuple-element.10.refs_1_, f32[4,128,2,32,128]{4,3,2,1,0:T(8,128)} %get-tuple-element.11.refs_2_, ...), custom_call_target="tpu_custom_call" | custom-call | tf_op jit(solution)/shard_map/pallas_call | solution.py:210
  97.1 12.6 %all_to_all.16 = f32[8,72,128]{2,1,0:T(8,128)S(1)} all-to-all(f32[8,72,128]{2,1,0:T(8,128)S(1)} %shard_map.59), channel_id=1, replica_groups=mesh['atom'=32,'kvec'=8] {'kvec'}, dimensions={0} | all-to-all | bytes 589824 | tf_op jit(solution)/shard_map/all_to_all | solution.py:221
  109.7 0.7 broadcast_in_dim.25
  110.4 4.8 %all-to-all-start.2 = ((f32[8,64,128]{2,1,0:T(8,128)}), f32[8,64,128]{2,1,0:T(8,128)S(1)}, u32[]{:S(2)}, u32[]{:S(2)}) async-start(f32[8,64,128]{2,1,0:T(8,128)} %broadcast_in_dim.25), calls=%async_computation.2 | async-start | bytes 524288 | tf_op jit(solution)/shard_map/all_to_all | solution.py:224
  115.2 0.5 slice.62
  115.8 5.3 %all-to-all-done.2 = f32[8,64,128]{2,1,0:T(8,128)S(1)} async-done(((f32[8,64,128]{2,1,0:T(8,128)}), f32[8,64,128]{2,1,0:T(8,128)S(1)}, u32[]{:S(2)}, u32[]{:S(2)}) %all-to-all-start.2) | async-done | bytes 262176 | tf_op jit(solution)/shard_map/all_to_all | solution.py:224
  121.2 0.7 slice_multiply_fusion
  121.9 0.8 multiply_multiply_fusion
  (15 shorter events, 0.2 us)
Async XLA Ops:
  3.4 0.8 copy-start
  44.9 21.1 %all-to-all-start = ((f32[32,1,1024]{2,1,0:T(1,128)}), f32[32,1,1024]{2,1,0:T(1,128)S(1)}, u32[]{:S(2)}, u32[]{:S(2)}) async-start(f32[32,1,1024]{2,1,0:T(1,128)} %broadcast_in_dim.24), calls=%async_computation | async-start | bytes 262144 | tf_op jit(solution)/shard_map/all_to_all | solution.py:203
  68.3 53.6 %copy-start.1 = (f32[16384]{0:T(1024)S(1)}, f32[16384]{0:T(1024)}, u32[]{:S(2)}) copy-start(f32[16384]{0:T(1024)} %param.4) | copy-start | bytes 196612
  110.4 10.6 %all-to-all-start.2 = ((f32[8,64,128]{2,1,0:T(8,128)}), f32[8,64,128]{2,1,0:T(8,128)S(1)}, u32[]{:S(2)}, u32[]{:S(2)}) async-start(f32[8,64,128]{2,1,0:T(8,128)} %broadcast_in_dim.25), calls=%async_computation.2 | async-start | bytes 524288 | tf_op jit(solution)/shard_map/all_to_all | solution.py:224

commit v3 on v0

v3 whole, which is shorter than its diff:
```python
import math

import jax
import jax.numpy as jnp
from jax import lax
from jax.experimental import pallas as pl
from jax.experimental.pallas import tpu as pltpu
from jax.sharding import PartitionSpec as P

TOP = 128
STRIDE = 16
BLOCK = 4096
ROWS = BLOCK // 128
HALF = ROWS // 2
PART = 32
SLOTS = 8
UNROLL = 8
MIB = 1 << 20


def rows_of(ref, start):
    return ref[pl.ds(pl.multiple_of(start, ROWS), ROWS), :]


def times(a, b):
    return a[0] * b[0] - a[1] * b[1], a[0] * b[1] + a[1] * b[0]


def turn(x):
    y = 4.0 * (x - jnp.round(x))
    n = jnp.round(y)
    r = (0.5 * math.pi) * (y - n)
    z = r * r
    s = r + r * z * (-1.6666654611e-1 + z * (8.3321608736e-3 - 1.9515295891e-4 * z))
    c = 4.166664568298827e-2 + z * (-1.388731625493765e-3 + 2.443315711809948e-5 * z)
    c = 1.0 + z * (c * z - 0.5)
    odd = jnp.abs(n) == 1.0
    cos = jnp.where(odd, s, c)
    sin = jnp.where(odd, c, s)
    cos = jnp.where((n > 0.5) | (n < -1.5), -cos, cos)
    sin = jnp.where((n > 1.5) | (n < -0.5), -sin, sin)
    return cos, sin


def fill_powers(x, low, cos_ref, sin_ref, signed):
    small = [(jnp.ones_like(x), jnp.zeros_like(x)), turn(x)]
    for b in range(2, STRIDE // 2 + 1):
        small.append(times(small[b // 2], small[b - b // 2]))
    big = times(small[-1], small[-1])

    def put(h, c, s):
        def at(r):
            return pl.ds(pl.multiple_of(r * ROWS + low, 8), HALF)

        cos_ref[at(h)] = c
        if signed:
            sin_ref[at(TOP + h)] = s
            sin_ref[at(TOP - h)] = -s
        else:
            sin_ref[at(h)] = s

    for b in range(STRIDE // 2):
        put(b, *small[b])

    def around(a, state, both):
        c, s = state
        put(STRIDE * a, c, s)
        for b in range(1, STRIDE // 2 + 1):
            cb, sb = small[b]
            cc, ss, sc, cs = c * cb, s * sb, s * cb, c * sb
            put(STRIDE * a - b, cc + ss, sc - cs)
            if both and b < STRIDE // 2:
                put(STRIDE * a + b, cc - ss, sc + cs)

    def step(a, state):
        around(a, state, True)
        return times(state, big)

    last = lax.fori_loop(1, TOP // STRIDE, step, big)
    around(TOP // STRIDE, last, False)


def eighths(v):
    return (v[0:8] + v[8:16]) + (v[16:24] + v[24:32])


def phases_kernel(idx_ref, xyz_ref, q_ref, e_ref, s_ref, xc, xs, yc, ys, zc, zs, acc, ring, sems):
    blocks, modes = e_ref.shape[0], e_ref.shape[1]
    parts = modes // PART

    def clear(i, carry):
        acc[i] = jnp.zeros((8, 128), jnp.float32)
        return carry

    lax.fori_loop(0, acc.shape[0], clear, 0, unroll=8)

    def copy(slot, b, p):
        return pltpu.make_async_copy(
            ring.at[slot], e_ref.at[b, pl.ds(p * PART, PART)], sems.at[slot]
        )

    def block(b, carry):
        for low in (0, HALF):
            for d, (c_ref, s_ref_) in enumerate(((xc, xs), (yc, ys), (zc, zs))):
                x = xyz_ref[d, pl.ds(pl.multiple_of(b * ROWS + low, HALF), HALF)]
                fill_powers(x, low, c_ref, s_ref_, d > 0)
        q = q_ref[pl.ds(pl.multiple_of(b * ROWS, ROWS), ROWS)]

        def part(p, carry):
            t = b * parts + p
            slot = lax.rem(t, SLOTS)

            @pl.when(t >= SLOTS)
            def _():
                copy(slot, b, p).wait()

            def mode(i, carry):
                k = p * PART + i
                at = k * 5
                h = idx_ref[at]
                first = rows_of(xc, h), rows_of(xs, h)
                second = rows_of(yc, idx_ref[at + 1]), rows_of(ys, idx_ref[at + 2])
                third = rows_of(zc, idx_ref[at + 3]), rows_of(zs, idx_ref[at + 4])
                c, s = times(times(first, second), third)
                ring[slot, i, 0] = c
                ring[slot, i, 1] = s
                acc[2 * k] += eighths(q * c)
                acc[2 * k + 1] += eighths(q * s)
                return carry

            lax.fori_loop(0, PART, mode, 0, unroll=UNROLL)
            copy(slot, b, p).start()
            return carry

        return lax.fori_loop(0, parts, part, carry)

    lax.fori_loop(0, blocks, block, 0)

    for at in range(0, 2 * modes, 128):
        rows = acc[at : at + 128, 0, :]
        for r in range(1, 8):
            rows = rows + acc[at : at + 128, r, :]
        line = jnp.sum(rows.T, axis=0, keepdims=True)
        s_ref[:, at : at + 128] = jnp.broadcast_to(line, (s_ref.shape[0], 128))

    def drain(slot, carry):
        copy(slot, 0, 0).wait()
        return carry

    lax.fori_loop(0, SLOTS, drain, 0)


def response_kernel(w_ref, e_ref, o_ref, ring, sems):
    blocks, modes = e_ref.shape[0], e_ref.shape[1]
    parts = modes // PART

    def copy(slot, b, p):
        return pltpu.make_async_copy(
            e_ref.at[b, pl.ds(p * PART, PART)], ring.at[slot], sems.at[slot]
        )

    def fetch(t):
        copy(lax.rem(t, SLOTS), t // parts, lax.rem(t, parts)).start()

    def first(t, carry):
        fetch(t)
        return carry

    lax.fori_loop(0, SLOTS, first, 0)
    zero = jnp.zeros((ROWS, 128), jnp.float32)

    def block(b, carry):
        def part(p, state):
            t = b * parts + p
            slot = lax.rem(t, SLOTS)
            copy(slot, b, p).wait()

            def mode(i, state):
                f0, f1, f2, pot = state
                at = (p * PART + i) * 5
                wr, wi = w_ref[at], w_ref[at + 1]
                c = ring[slot, i, 0]
                s = ring[slot, i, 1]
                pot = pot + (wr * c + wi * s)
                g = wr * s - wi * c
                return (
                    f0 + w_ref[at + 2] * g,
                    f1 + w_ref[at + 3] * g,
                    f2 + w_ref[at + 4] * g,
                    pot,
                )

            state = lax.fori_loop(0, PART, mode, state, unroll=UNROLL)

            @pl.when(t + SLOTS < blocks * parts)
            def _():
                fetch(t + SLOTS)

            return state

        state = lax.fori_loop(0, parts, part, (zero,) * 4)
        for t in range(2):
            for c in range(4):
                o_ref[2 * b + t, HALF * c : HALF * (c + 1)] = state[c][HALF * t : HALF * (t + 1)]
            o_ref[2 * b + t, 4 * HALF :] = jnp.full((8, 128), w_ref[5 * modes], jnp.float32)
        return carry

    lax.fori_loop(0, blocks, block, 0)


def on_device(scaled_coordinate_array, particle_charge_list, reciprocal_triples):
    local_atoms = scaled_coordinate_array.shape[1]
    modes = reciprocal_triples.shape[1]
    n_atom = lax.axis_size("atom")
    n_kvec = lax.axis_size("kvec")
    natoms = local_atoms * n_atom
    blocks = local_atoms // BLOCK

    triples = reciprocal_triples * jnp.where(reciprocal_triples[0:1] < 0, -1, 1)
    table = 2.0 * math.pi * triples.astype(jnp.float32)
    norm = jnp.sum(table * table, axis=0)
    damping = 4.0 * math.pi * jnp.exp(-norm / 1600000.0) / norm
    idx = ROWS * jnp.stack(
        [
            triples[0],
            jnp.abs(triples[1]),
            triples[1] + TOP,
            jnp.abs(triples[2]),
            triples[2] + TOP,
        ],
        axis=1,
    ).reshape(5 * modes)
    xyz = scaled_coordinate_array.reshape(3, local_atoms // 128, 128)
    q = particle_charge_list.reshape(local_atoms // 128, 128)

    smem = pl.BlockSpec(memory_space=pltpu.SMEM)
    vmem = pl.BlockSpec(memory_space=pltpu.VMEM)
    hbm = pl.BlockSpec(memory_space=pl.ANY)
    ring = [
        pltpu.VMEM((SLOTS, PART, 2, ROWS, 128), jnp.float32),
        pltpu.SemaphoreType.DMA((SLOTS,)),
    ]
    positive = pltpu.VMEM(((TOP + 1) * ROWS, 128), jnp.float32)
    both = pltpu.VMEM(((2 * TOP + 1) * ROWS, 128), jnp.float32)
    e, share = pl.pallas_call(
        phases_kernel,
        in_specs=[smem, vmem, vmem],
        out_specs=[hbm, vmem],
        out_shape=[
            jax.ShapeDtypeStruct((blocks, modes, 2, ROWS, 128), jnp.float32),
            jax.ShapeDtypeStruct((n_atom, 2 * modes), jnp.float32),
        ],
        scratch_shapes=[
            positive,
            positive,
            positive,
            both,
            positive,
            both,
            pltpu.VMEM((2 * modes, 8, 128), jnp.float32),
        ]
        + ring,
        compiler_params=pltpu.CompilerParams(vmem_limit_bytes=48 * MIB),
    )(idx, xyz, q)

    total = lax.all_to_all(share, "atom", 0, 0, tiled=True).sum(axis=0)
    total = total.reshape(modes, 2)
    cosine, sine = total[:, 0], total[:, 1]
    partial_energy = 50.0 / natoms * jnp.sum(damping * (cosine * cosine + sine * sine))
    w = jnp.concatenate([(damping * cosine)[None], (damping * sine)[None], table])
    w = jnp.concatenate([w.T.reshape(5 * modes), partial_energy.reshape(1)])

    terms = pl.pallas_call(
        response_kernel,
        in_specs=[smem, hbm],
        out_specs=vmem,
        out_shape=jax.ShapeDtypeStruct((n_kvec, 4 * HALF + 8, 128), jnp.float32),
        scratch_shapes=ring,
        compiler_params=pltpu.CompilerParams(vmem_limit_bytes=24 * MIB),
    )(w, e)

    own = lax.all_to_all(terms, "kvec", 0, 0, tiled=True).sum(axis=0)
    energy = own[4 * HALF, 0]
    copies = jnp.broadcast_to(own[None, : 4 * HALF], (n_kvec, 4 * HALF, 128))
    summed = lax.all_to_all(copies, "kvec", 0, 0, tiled=True)
    summed = summed.reshape(n_kvec, 4, HALF * 128).transpose(1, 0, 2).reshape(4, local_atoms)
    scale = 1.0 / math.sqrt(natoms)
    forces = summed[:3] * particle_charge_list[None, :] * scale
    potential = summed[3] * (400.0 * scale)
    return (forces, potential, energy)


def solution(mesh):
    return jax.shard_map(
        on_device,
        mesh=mesh,
        in_specs=(P(None, "atom"), P("atom"), P(None, "kvec")),
        out_specs=(P(None, "atom"), P("atom"), P()),
        check_vma=False,
    )
```

time: 303 us -> 107 us (0.35)
  other arithmetic: 141 us -> 4.13 us
  matrix products: 104 us -> 0 us
  Pallas kernels: 0 us -> 52.6 us
  blocking collectives: 32 us -> 12.6 us
  waiting for transfers between devices: 10.7 us -> 16 us
  starting transfers between devices: 10.6 us -> 15.2 us
    dynamic_update_slice x4 -> x0, other arithmetic: 135 us -> none  [on_device(): cos_tile, sin_tile = lax.map(make_tiles, tile_blocks)]
    dot_general x4 -> x0, matrix products: 104 us -> none  [the longest x1 30.9 us: on_device(): jnp.dot(sin_tile, sine_lookup, precision=largest_wave_index, preferred_el...]
    pallas_call x0 -> x2, Pallas kernels: none -> 52.6 us  [the longest x1 31.1 us: on_device(): pl.pallas_call(phases_kernel, in_specs=[smem, vmem, vmem], out_specs=[hbm...]
    all_to_all x1, blocking collectives: 32 us -> 12.6 us  [on_device(): own = lax.all_to_all(terms, 'kvec', 0, 0, tiled=True).sum(axis=0)]
    all_to_all x1 -> x2, waiting for transfers between devices: 10.7 us -> 16 us  [the longest x1 10.7 us: on_device(): total = lax.all_to_all(share, 'atom', 0, 0, tiled=True).sum(axis=0)]
    all_to_all x1 -> x2, starting transfers between devices: 10.6 us -> 15.2 us  [the longest x1 10.4 us: on_device(): total = lax.all_to_all(share, 'atom', 0, 0, tiled=True).sum(axis=0)]
  transfers between devices with their start and end apart: 1 -> 2, of which waited for: 1 -> 2; matrix products, arithmetic and copies ran while one was open for 0% -> 0% of each run, Pallas kernels for 0% -> 0%
where the time goes in v3:
time: 107 us
  Pallas kernels  52.6 us (49%)
  waiting for transfers between devices  16 us (15%)
  starting transfers between devices  15.2 us (14%)
  blocking collectives  12.6 us (12%)
  local copies, waits for them, and re-layouts  4.86 us (5%)
  other arithmetic  4.13 us (4%)
  between operations  1.41 us (1%)
    pallas_call x1, Pallas kernels, on_device(): pl.pallas_call(phases_kernel, in_specs=[smem, vmem, vmem], out_specs=[hbm...  31.1 us
    pallas_call x1, Pallas kernels, on_device(): pl.pallas_call(response_kernel, in_specs=[smem, hbm], out_specs=vmem, out...  21.5 us
    all_to_all x1, blocking collectives, on_device(): own = lax.all_to_all(terms, 'kvec', 0, 0, tiled=True).sum(axis=0)  12.6 us
    all_to_all x1, waiting for transfers between devices, on_device(): total = lax.all_to_all(share, 'atom', 0, 0, tiled=True).sum(axis=0)  10.7 us
    all_to_all x1, starting transfers between devices, on_device(): total = lax.all_to_all(share, 'atom', 0, 0, tiled=True).sum(axis=0)  10.4 us
    all_to_all x1, waiting for transfers between devices, on_device(): summed = lax.all_to_all(copies, 'kvec', 0, 0, tiled=True)  5.33 us
    all_to_all x1, starting transfers between devices, on_device(): summed = lax.all_to_all(copies, 'kvec', 0, 0, tiled=True)  4.8 us
  transfers between devices with their start and end apart: 2, of which 2 were waited for; matrix products, arithmetic and copies ran while one was open for 0% of the time, Pallas kernels for 0%

profile of v3, /device:TPU:2, one launch (start us, length us, event | category | flops | bytes accessed | tf_op | source)
XLA Modules:
  0.0 106.8 jit_solution(7804376321128362543)
XLA Ops:
  0.6 0.7 compare_select_fusion
  1.4 0.7 convert_multiply_fusion
  2.1 1.0 copy.13
  3.1 0.1 copy.8
  3.3 0.2 mul.112.idx_ref
  3.5 0.8 copy-done
  4.3 31.1 %shard_map.58 = (f32[4,512,2,32,128]{4,3,2,1,0:T(8,128)}, f32[32,1024]{1,0:T(8,128)S(1)}) custom-call(s32[2560]{0:T(1024)S(1)} %mul.112.idx_ref, f32[3,128,128]{2,1,0:T(8,128)S(1)} %bitcast.28, f32[128,128]{1,0:T(8,128)S(1)} %bitcast.29), custom_call_target="tpu_custom_call" | custom-call | tf_op jit(solution)/shard_map/pallas_call | solution.py:245
  35.4 0.8 copy.9
  36.2 10.4 %all-to-all-start = ((f32[32,1,1024]{2,1,0:T(1,128)}), f32[32,1,1024]{2,1,0:T(1,128)S(1)}, u32[]{:S(2)}, u32[]{:S(2)}) async-start(f32[32,1,1024]{2,1,0:T(1,128)} %copy.9), calls=%async_computation | async-start | bytes 262144 | tf_op jit(solution)/shard_map/all_to_all | solution.py:266
  46.6 10.7 %all-to-all-done = f32[32,1,1024]{2,1,0:T(1,128)S(1)} async-done(((f32[32,1,1024]{2,1,0:T(1,128)}), f32[32,1,1024]{2,1,0:T(1,128)S(1)}, u32[]{:S(2)}, u32[]{:S(2)}) %all-to-all-start) | async-done | bytes 131104 | tf_op jit(solution)/shard_map/all_to_all | solution.py:266
  57.3 0.1 reduce_sum.40
  57.4 0.2 reshape.131
  57.6 0.4 slice_reduce_fusion.1
  58.0 0.6 multiply_reduce_fusion.1
  58.7 0.1 copy.10
  58.8 0.2 reshape.132
  59.7 21.5 %shard_map.59 = f32[8,72,128]{2,1,0:T(8,128)S(1)} custom-call(f32[2561]{0:T(1024)S(1)} %pad_maximum_fusion.w_ref, f32[4,512,2,32,128]{4,3,2,1,0:T(8,128)} %get-tuple-element.6.e_ref), custom_call_target="tpu_custom_call" | custom-call | tf_op jit(solution)/shard_map/pallas_call | solution.py:273
  81.2 12.6 %all_to_all.19 = f32[8,72,128]{2,1,0:T(8,128)S(1)} all-to-all(f32[8,72,128]{2,1,0:T(8,128)S(1)} %shard_map.59), channel_id=1, replica_groups=mesh['atom'=32,'kvec'=8] {'kvec'}, dimensions={0} | all-to-all | bytes 589824 | tf_op jit(solution)/shard_map/all_to_all | solution.py:282
  93.8 0.7 broadcast_in_dim.19
  94.5 4.8 %all-to-all-start.2 = ((f32[8,64,128]{2,1,0:T(8,128)}), f32[8,64,128]{2,1,0:T(8,128)S(1)}, u32[]{:S(2)}, u32[]{:S(2)}) async-start(f32[8,64,128]{2,1,0:T(8,128)} %broadcast_in_dim.19), calls=%async_computation.2 | async-start | bytes 524288 | tf_op jit(solution)/shard_map/all_to_all | solution.py:285
  99.3 0.5 slice.55
  99.8 5.3 %all-to-all-done.2 = f32[8,64,128]{2,1,0:T(8,128)S(1)} async-done(((f32[8,64,128]{2,1,0:T(8,128)}), f32[8,64,128]{2,1,0:T(8,128)S(1)}, u32[]{:S(2)}, u32[]{:S(2)}) %all-to-all-start.2) | async-done | bytes 262176 | tf_op jit(solution)/shard_map/all_to_all | solution.py:285
  105.3 0.7 slice_multiply_fusion
  106.0 0.8 multiply_multiply_fusion
  (14 shorter events, 0.2 us)
Async XLA Ops:
  0.6 105.4 %copy-start.1 = (f32[16384]{0:T(1024)S(1)}, f32[16384]{0:T(1024)}, u32[]{:S(2)}) copy-start(f32[16384]{0:T(1024)} %param.4) | copy-start | bytes 196612
  3.5 0.8 copy-start
  36.2 21.1 %all-to-all-start = ((f32[32,1,1024]{2,1,0:T(1,128)}), f32[32,1,1024]{2,1,0:T(1,128)S(1)}, u32[]{:S(2)}, u32[]{:S(2)}) async-start(f32[32,1,1024]{2,1,0:T(1,128)} %copy.9), calls=%async_computation | async-start | bytes 262144 | tf_op jit(solution)/shard_map/all_to_all | solution.py:266
  94.5 10.6 %all-to-all-start.2 = ((f32[8,64,128]{2,1,0:T(8,128)}), f32[8,64,128]{2,1,0:T(8,128)S(1)}, u32[]{:S(2)}, u32[]{:S(2)}) async-start(f32[8,64,128]{2,1,0:T(8,128)} %broadcast_in_dim.19), calls=%async_computation.2 | async-start | bytes 524288 | tf_op jit(solution)/shard_map/all_to_all | solution.py:285
